TPU v7x, 32 devices: a 4x4x1 block of a 4x4x8 slice. The times are simulated.
32 devices in a mesh: rep: 2 (over z, core), dp: 16 (over x, y).
Axes of the slice: x: 4, y: 4, z: 1, core: 2. Of those that a mesh axis runs over, the one named last changes fastest.
The devices are a block of a 4x4x8 slice.
Arguments:
- g_w_gate: bfloat16 [32, 2, 1536, 4224], P(('rep', 'dp')), parts along dimension 0
- g_w_up: bfloat16 [32, 2, 1536, 4224], P(('rep', 'dp')), parts along dimension 0
- g_w_down: bfloat16 [32, 2, 4224, 1536], P(('rep', 'dp')), parts along dimension 0
- w_gate: bfloat16 [2, 1536, 4224], replicated
- w_up: bfloat16 [2, 1536, 4224], replicated
- w_down: bfloat16 [2, 4224, 1536], replicated
- m_w_gate: float32 [2, 1536, 4224], P(None, 'dp')
- m_w_up: float32 [2, 1536, 4224], P(None, 'dp')
- m_w_down: float32 [2, 4224, 1536], P(None, 'dp')
- v_w_gate: float32 [2, 1536, 4224], P(None, 'dp')
- v_w_up: float32 [2, 1536, 4224], P(None, 'dp')
- v_w_down: float32 [2, 4224, 1536], P(None, 'dp')
Outputs:
- output 1: bfloat16 [4, 1536, 4224], P('rep'), parts along dimension 0
- output 2: bfloat16 [4, 1536, 4224], P('rep'), parts along dimension 0
- output 3: bfloat16 [4, 4224, 1536], P('rep'), parts along dimension 0
- output 4: float32 [4, 1536, 4224], P('rep', 'dp'), parts along dimension 0
- output 5: float32 [4, 1536, 4224], P('rep', 'dp'), parts along dimension 0
- output 6: float32 [4, 4224, 1536], P('rep', 'dp'), parts along dimension 0
- output 7: float32 [4, 1536, 4224], P('rep', 'dp'), parts along dimension 0
- output 8: float32 [4, 1536, 4224], P('rep', 'dp'), parts along dimension 0
- output 9: float32 [4, 4224, 1536], P('rep', 'dp'), parts along dimension 0
There are 2 independent parts. A program takes and returns all parts, laid end to end along the dimension named above; an argument that names none is the same for every part.
All inputs are finite; a program needn't handle non-finite values.
Results may differ from a plain program's by a relative error of at most 0.022.
Values are sent between devices in bfloat16 or wider.
A program may use at most 768 MiB of HBM per device.

v0:
```python
import jax
import jax.numpy as jnp
from jax import lax
from jax.sharding import PartitionSpec as P


def adamw(w, m, v, g):
    m = 0.9 * m + 0.1 * g
    v = 0.95 * v + 0.05 * g * g
    step = m * lax.rsqrt(v + 1e-8) + 0.1 * w
    return (w - 0.02 * step).astype(jnp.bfloat16), m, v


def clipped(gradients, sum_of_squares, count):
    factor = jnp.minimum(1.0, 0.5 * lax.rsqrt(sum_of_squares / count + 1e-30))
    return [g * factor for g in gradients]


def solution(mesh):
    def step(*arrays):
        terms, weights, m, v = (arrays[i : i + 3] for i in (0, 3, 6, 9))
        gradients = [lax.psum_scatter(t[0], "dp", scatter_dimension=1, tiled=True).astype(jnp.float32) for t in terms]
        squares = lax.psum(sum(jnp.sum(g * g) for g in gradients), "dp")
        gradients = clipped(gradients, squares, lax.psum(1, "dp") * sum(g.size for g in gradients))
        me = lax.axis_index("dp")
        own = [lax.dynamic_slice_in_dim(w, me * one.shape[1], one.shape[1], 1).astype(jnp.float32) for w, one in zip(weights, m, strict=True)]
        new = [adamw(w, m, v, g) for w, m, v, g in zip(own, m, v, gradients, strict=True)]
        whole = [lax.all_gather(one[0], "dp", axis=1, tiled=True) for one in new]
        return (*whole, *(one[1] for one in new), *(one[2] for one in new))

    all_of, cut = P(None, None, None), P(None, "dp", None)
    return jax.shard_map(
        step,
        mesh=mesh,
        in_specs=(P(("rep", "dp"), None, None, None),) * 3 + (all_of,) * 3 + (cut,) * 6,
        out_specs=(P("rep", None, None),) * 3 + (P("rep", "dp", None),) * 6,
        check_vma=False,
    )
```

profile of v0, /device:TPU:97, one launch (start us, length us, event | category | flops | bytes accessed | tf_op | source)
XLA Modules:
  0.0 1199.8 jit_solution(9206313996979137418)
XLA Ops:
  7.2 0.1 all-reduce.3.cloned.1.call-start
  7.3 0.7 all-reduce.3.cloned.1.call-update
  8.0 0.1 reduce-scatter.4.cloned.1.call-start
  8.1 0.7 reduce-scatter.4.cloned.1.call-update
  8.8 0.1 reduce-scatter.6.cloned.1.call-start
  8.9 0.0 copy-start.2
  8.9 0.7 reduce-scatter.6.cloned.1.call-update
  9.6 0.1 all-gather.8.cloned.1.call-start
  9.7 0.0 copy-done.2
  9.7 0.6 dynamic-slice
  10.9 306.5 %all-reduce.3.cloned.1.call-done = bf16[2,4224,1536]{2,1,0:T(8,128)(2,1)} async-done(((bf16[2,4224,1536]{2,1,0:T(8,128)(2,1)}), bf16[2,4224,1536]{2,1,0:T(8,128)(2,1)}) %all-reduce.3.cloned.1.call-update) | async-done | bytes 25952272
  317.4 2.9 fusion.11
  320.2 152.2 %reduce-scatter.4.cloned.1.call-done = bf16[2,96,4224]{2,1,0:T(8,128)(2,1)} async-done(((bf16[2,1536,4224]{2,1,0:T(8,128)(2,1)}), bf16[2,96,4224]{2,1,0:T(8,128)(2,1)}) %reduce-scatter.4.cloned.1.call-update) | async-done | bytes 1622032 | tf_op jit(solution)/shard_map/reduce_scatter | solution.py:22
  472.4 2.9 fusion.9
  475.3 152.1 %reduce-scatter.6.cloned.1.call-done = bf16[2,96,4224]{2,1,0:T(8,128)(2,1)} async-done(((bf16[2,1536,4224]{2,1,0:T(8,128)(2,1)}), bf16[2,96,4224]{2,1,0:T(8,128)(2,1)}) %reduce-scatter.6.cloned.1.call-update) | async-done | bytes 1622032 | tf_op jit(solution)/shard_map/reduce_scatter | solution.py:22
  627.3 2.9 fusion.10
  632.1 31.7 %psum.7 = f32[]{:T(128)} all-reduce(f32[]{:T(128)S(6)} %add.65), channel_id=1, replica_groups=mesh['rep'=2,'dp'=16] {'dp'}, use_global_device_ids=true, to_apply=%region_6.0 | all-reduce | flops 1 | bytes 8 | tf_op jit(solution)/shard_map/psum | solution.py:23
  664.6 0.0 copy-start.1
  664.6 6.5 fusion.17
  671.0 0.1 all-gather.8.cloned.1.call-update
  671.1 0.1 all-gather.4.cloned.1.call-start
  671.2 0.0 copy-done.1
  671.2 0.0 copy-start
  671.2 5.9 fusion.8
  677.1 0.1 all-gather.4.cloned.1.call-update
  677.2 0.1 all-gather.6.cloned.1.call-start
  677.3 0.0 copy-done
  677.3 5.8 fusion.14
  683.1 0.1 all-gather.6.cloned.1.call-update
  683.2 144.1 %all-gather.8.cloned.1.call-done = bf16[2,4224,1536]{2,1,0:T(8,128)(2,1)} async-done(((bf16[2,264,1536]{2,1,0:T(8,128)(2,1)}), bf16[2,4224,1536]{2,1,0:T(8,128)(2,1)}) %all-gather.8.cloned.1.call-update) | async-done | bytes 25952272 | tf_op jit(solution)/shard_map/all_gather | solution.py:28
  827.3 155.0 %all-gather.4.cloned.1.call-done = bf16[2,1536,4224]{2,1,0:T(8,128)(2,1)} async-done(((bf16[2,96,4224]{2,1,0:T(8,128)(2,1)}), bf16[2,1536,4224]{2,1,0:T(8,128)(2,1)}) %all-gather.4.cloned.1.call-update) | async-done | bytes 25952272 | tf_op jit(solution)/shard_map/all_gather | solution.py:28
  982.3 155.0 %all-gather.6.cloned.1.call-done = bf16[2,1536,4224]{2,1,0:T(8,128)(2,1)} async-done(((bf16[2,96,4224]{2,1,0:T(8,128)(2,1)}), bf16[2,1536,4224]{2,1,0:T(8,128)(2,1)}) %all-gather.6.cloned.1.call-update) | async-done | bytes 25952272 | tf_op jit(solution)/shard_map/all_gather | solution.py:28
  1137.3 0.0 slice-start
  1137.3 0.0 slice-start.1
  1137.3 0.0 slice-start.2
  1137.3 0.0 slice-start.3
  1137.3 23.8 %copy.28 = bf16[2,1536,4224]{2,1,0:T(8,128)(2,1)} copy(bf16[2,1536,4224]{2,1,0:T(8,128)(2,1)} %all-gather.4.cloned.1.call-done) | data formatting | bytes 51904512
  1161.1 0.0 slice-start.4
  1161.2 0.0 slice-start.5
  1161.2 22.6 %copy.29 = bf16[2,1536,4224]{2,1,0:T(8,128)(2,1)} copy(bf16[2,1536,4224]{2,1,0:T(8,128)(2,1)} %all-gather.6.cloned.1.call-done) | data formatting | bytes 51904512
  1183.7 0.0 slice-done
  1183.7 0.0 slice-done.1
  1183.7 0.0 slice-done.2
  1183.7 0.0 slice-done.3
  1183.7 0.0 slice-done.4
  1183.7 0.0 slice-done.5
  1183.8 0.0 slice-done.6
  1183.8 9.2 copy.30
  (2 shorter events, 0.0 us)
Async XLA Ops:
  7.2 310.2 %all-reduce.3.cloned.1.call-start = ((), (), s32[]{:S(2)}) async-start(), calls=%async_computation.7 | async-start | bytes 51904512
  8.0 464.4 %reduce-scatter.4.cloned.1.call-start = ((), (), s32[]{:S(2)}) async-start(), calls=%async_computation.2 | async-start | bytes 27574272 | tf_op jit(solution)/shard_map/reduce_scatter | solution.py:22
  8.8 618.5 %reduce-scatter.6.cloned.1.call-start = ((), (), s32[]{:S(2)}) async-start(), calls=%async_computation.3 | async-start | bytes 27574272 | tf_op jit(solution)/shard_map/reduce_scatter | solution.py:22
  8.9 0.8 copy-start.2
  9.6 817.7 %all-gather.8.cloned.1.call-start = ((), (), s32[]{:S(2)}) async-start(), calls=%async_computation.6 | async-start | bytes 27574272 | tf_op jit(solution)/shard_map/all_gather | solution.py:28
  664.6 6.6 copy-start.1
  671.1 311.2 %all-gather.4.cloned.1.call-start = ((), (), s32[]{:S(2)}) async-start(), calls=%async_computation.4 | async-start | bytes 27574272 | tf_op jit(solution)/shard_map/all_gather | solution.py:28
  671.2 6.1 copy-start
  677.2 460.1 %all-gather.6.cloned.1.call-start = ((), (), s32[]{:S(2)}) async-start(), calls=%async_computation.5 | async-start | bytes 27574272 | tf_op jit(solution)/shard_map/all_gather | solution.py:28
  1137.3 46.4 %slice-start = ((s8[25952256]{0:T(1024)(128)(4,1)}), s8[4194304]{0:T(1024)(128)(4,1)S(1)}, s32[]{:S(2)}) async-start(s8[25952256]{0:T(1024)(128)(4,1)} %bitcast.9), calls=%async_computation.8 | async-start | bytes 8388608
  1137.3 46.4 %slice-start.1 = ((s8[25952256]{0:T(1024)(128)(4,1)}), s8[4194304]{0:T(1024)(128)(4,1)S(1)}, s32[]{:S(2)}) async-start(s8[25952256]{0:T(1024)(128)(4,1)} %bitcast.9), calls=%async_computation.9 | async-start | bytes 8388608
  1137.3 46.4 %slice-start.2 = ((s8[25952256]{0:T(1024)(128)(4,1)}), s8[4194304]{0:T(1024)(128)(4,1)S(1)}, s32[]{:S(2)}) async-start(s8[25952256]{0:T(1024)(128)(4,1)} %bitcast.9), calls=%async_computation.10 | async-start | bytes 8388608
  1137.3 46.4 %slice-start.3 = ((s8[25952256]{0:T(1024)(128)(4,1)}), s8[4194304]{0:T(1024)(128)(4,1)S(1)}, s32[]{:S(2)}) async-start(s8[25952256]{0:T(1024)(128)(4,1)} %bitcast.9), calls=%async_computation.11 | async-start | bytes 8388608
  1161.1 22.6 %slice-start.4 = ((s8[25952256]{0:T(1024)(128)(4,1)}), s8[4194304]{0:T(1024)(128)(4,1)S(1)}, s32[]{:S(2)}) async-start(s8[25952256]{0:T(1024)(128)(4,1)} %bitcast.9), calls=%async_computation.12 | async-start | bytes 8388608
  1161.2 22.6 %slice-start.5 = ((s8[25952256]{0:T(1024)(128)(4,1)}), s8[4194304]{0:T(1024)(128)(4,1)S(1)}, s32[]{:S(2)}) async-start(s8[25952256]{0:T(1024)(128)(4,1)} %bitcast.9), calls=%async_computation.13 | async-start | bytes 8388608
  1161.2 22.6 %slice-start.6 = ((s8[25952256]{0:T(1024)(128)(4,1)}), s8[786432]{0:T(1024)(128)(4,1)S(1)}, s32[]{:S(2)}) async-start(s8[25952256]{0:T(1024)(128)(4,1)} %bitcast.9), calls=%async_computation.14 | async-start | bytes 1572864
Sparse Core Ops, SparseCore 0:
  11.8 305.5 all-reduce.2
  320.7 151.6 reduce-scatter.3
  475.7 151.5 reduce-scatter.5
  671.2 156.0 all-gather.7
  829.7 152.5 all-gather.3
  984.7 152.5 all-gather.5
where the time goes:
time: 1200 us
  waiting for transfers between devices  1070 us (89%)
  local copies, waits for them, and re-layouts  56.2 us (5%)
  blocking collectives  31.7 us (3%)
  other arithmetic  26.8 us (2%)
  between operations  17.5 us (1%)
    all_gather x3, waiting for transfers between devices, step(): whole = [lax.all_gather(one[0], 'dp', axis=1, tiled=True) for one in new]  454 us
    unnamed x7, waiting for transfers between devices  309 us
    reduce_scatter x2, waiting for transfers between devices, step(): lax.psum_scatter(t[0], 'dp', scatter_dimension=1, tiled=True)  304 us
    unnamed x24, local copies, waits for them, and re-layouts  56.2 us
    psum x1, blocking collectives, step(): squares = lax.psum(sum((jnp.sum(g * g) for g in gradients)), 'dp')  31.7 us
  transfers between devices with their start and end apart: 6, of which 6 were waited for; matrix products, arithmetic and copies ran while one was open for 2% of the time, Pallas kernels for 0%

commit v1 on v0

v1 whole, which is shorter than its diff:
```python
import functools
import math

import jax
import jax.numpy as jnp
from jax import lax
from jax.experimental import pallas as pl
from jax.experimental.pallas import tpu as pltpu
from jax.sharding import PartitionSpec as P

MESH = pl.DeviceIdType.MESH
F32, BF16 = jnp.float32, jnp.bfloat16
COLOURS = range(4)
PIECES = 4


def divisor(whole, unit, most):
    return max(d for d in range(unit, most + 1, unit) if whole % d == 0)


def moments(m, v, g):
    m = 0.9 * m + 0.1 * g
    v = 0.95 * v + 0.05 * g * g
    return m, v


def new_weight(w, m, v):
    step = m * lax.rsqrt(v + 1e-8) + 0.1 * w
    return (w - 0.02 * step).astype(BF16)


def kernel(n, side, count,
           g_gate, g_up, g_down, w_gate, w_up, w_down, m_gate, m_up, m_down, v_gate, v_up, v_down,
           o_gate, o_up, o_down, og_gate, og_up, og_down, factor_ref,
           bufr, bufc, ownr, ownc, mr, mc, vr, vc, acc, sq,
           ss, rs, own_sem, mv_sem, cred1, cred2, sq_ss, sq_rs, loc_sem, ags_a, agr_a, ags_b, agr_b, agr_own, ags_own):
    layers = g_gate.shape[0]
    r, wide = bufr.shape[-2:]
    tall, quarter = bufc.shape[-2:]
    cstep = divisor(wide, 128, 384)
    rstep = divisor(tall, 8, 24)
    kinds = PIECES + layers

    me = lax.axis_index("dp")
    x, y = me // side, lax.rem(me, side)

    def around(v):
        return lax.rem(v + 4 * side, side)

    def ab(c):
        return (x, y) if c < 2 else (y, x)

    def sign(c):
        return 1 if c % 2 == 0 else -1

    def dev(c, a, b):
        return a * side + b if c < 2 else b * side + a

    def to(device):
        return {"dp": device}

    def along_a(c, k):
        a, b = ab(c)
        return dev(c, around(a + k * sign(c)), b)

    def along_b(c, k):
        a, b = ab(c)
        return dev(c, a, around(b + k * sign(c)))

    def block(c, back_a, back_b):
        a, b = ab(c)
        return dev(c, around(a - back_a * sign(c)), around(b - back_b * sign(c)))

    gates = (g_gate, g_up), (w_gate, w_up), (m_gate, m_up), (v_gate, v_up), (o_gate, o_up), (og_gate, og_up)

    def pick(which, c):
        return gates[which][c // layers], c % layers

    def cols(c):
        return pl.ds(c * quarter, quarter)

    def source(which, down, c, j, i):
        if i < PIECES:
            ref, layer = pick(which, c)
            return ref.at[layer, j, i]
        return down.at[i - PIECES, j, :, cols(c)]

    def part(r_ref, c_ref, lead, i):
        return r_ref.at[(*lead, i)] if i < PIECES else c_ref.at[(*lead, i - PIECES)]

    def buf(par, c, q, i):
        return part(bufr, bufc, (par, c, q), i)

    def own(par, c, i):
        return part(ownr, ownc, (par, c), i)

    def copy(src, dst, send, recv, device):
        return pltpu.make_async_remote_copy(src, dst, send, recv, device_id=to(device), device_id_type=MESH)

    def got(ref, sem):
        pltpu.make_async_copy(ref, ref, sem).wait()

    barrier = pltpu.get_barrier_semaphore()
    for k in range(1, n):
        pl.semaphore_signal(barrier, inc=1, device_id=to(lax.rem(me + k, n)), device_id_type=MESH)
    pl.semaphore_wait(barrier, n - 1)

    @pl.loop(0, side)
    def _(q):
        for i in range(kinds):
            for c in COLOURS:
                copy(source(0, g_down, c, block(c, 1, q + 1), i), buf(0, c, q, i), ss.at[0, c, q, i], rs.at[0, c, q, i], along_a(c, 1)).start()

    def own_load(step, which, down, c, i):
        stage, q = 1 + step // side, lax.rem(step, side)
        j = block(c, stage + 1, q + 1)
        par = lax.rem(step, 2)
        return pltpu.make_async_copy(source(which, down, c, j, i), own(par, c, i), own_sem.at[par, c, i])

    def start_own(step):
        for i in range(kinds):
            for c in COLOURS:
                own_load(step, 0, g_down, c, i).start()

    def mv_load(c, i):
        if i < PIECES:
            (m, layer), (v, _) = pick(2, c), pick(3, c)
            srcs = m.at[layer, i], v.at[layer, i]
        else:
            srcs = m_down.at[i - PIECES, :, cols(c)], v_down.at[i - PIECES, :, cols(c)]
        dsts = part(mr, mc, (c,), i), part(vr, vc, (c,), i)
        if i < PIECES:
            dsts = mr.at[c, i % 2], vr.at[c, i % 2]
        return [pltpu.make_async_copy(s, d, mv_sem.at[k, c, i]) for k, (s, d) in enumerate(zip(srcs, dsts, strict=True))]

    start_own(0)
    for i in (0, 1, *range(PIECES, kinds)):
        for c in COLOURS:
            for cp in mv_load(c, i):
                cp.start()

    def tiles(i, body):
        if i < PIECES:
            @pl.loop(0, wide // cstep)
            def _(k):
                body((slice(None), pl.ds(pl.multiple_of(k * cstep, 128), cstep)))
        else:
            @pl.loop(0, tall // rstep)
            def _(k):
                body((pl.ds(pl.multiple_of(k * rstep, 8), rstep), slice(None)))

    def add(i, dst, *more):
        def body(at):
            total = dst[at].astype(F32)
            for one in more:
                total += one[at].astype(F32)
            dst[at] = total.astype(BF16)

        tiles(i, body)

    @pl.loop(0, 2 * side)
    def _(step):
        par, q = step // side, lax.rem(step, side)
        start_own(step + 1)
        for i in range(kinds):
            for c in COLOURS:
                got(buf(par, c, q, i), rs.at[par, c, q, i])
                got(buf(par, c, q, i), ss.at[par, c, q, i])

                @pl.when(par == 1)
                def _():
                    pl.semaphore_signal(cred1.at[c], inc=1, device_id=to(along_a(c, -1)), device_id_type=MESH)

                own_load(step, 0, g_down, c, i).wait()
                add(i, buf(par, c, q, i), own(lax.rem(step, 2), c, i))
            for c in COLOURS:
                @pl.when(par == 1)
                def _():
                    pl.semaphore_wait(cred1.at[c], 1)

                copy(buf(par, c, q, i), buf(1 - par, c, q, i), ss.at[1 - par, c, q, i], rs.at[1 - par, c, q, i], along_a(c, 1)).start()

    acc[...] = jnp.zeros_like(acc)
    for q in range(side):
        step = 2 * side + q
        if q < side - 1:
            start_own(step + 1)
        else:
            for i in range(kinds):
                for c in COLOURS:
                    own_load(step + 1, 1, w_down, c, i).start() if False else None
                    pltpu.make_async_copy(source(1, w_down, c, me, i), own((step + 1) % 2, c, i), own_sem.at[(step + 1) % 2, c, i]).start()
        for i in range(kinds):
            for c in COLOURS:
                here = buf(0, c, q, i)
                got(here, rs.at[0, c, q, i])
                got(here, ss.at[0, c, q, i])
                if q < side - 1:
                    pl.semaphore_signal(cred2.at[c], inc=1, device_id=to(along_b(c, -1)), device_id_type=MESH)
                own_load(step, 0, g_down, c, i).wait()
                more = [own(step % 2, c, i)]
                if q:
                    got(here, rs.at[1, c, q - 1, i])
                    got(here, ss.at[1, c, q - 1, i])
                    more.append(buf(1, c, q - 1, i))
                if q < side - 1:
                    add(i, here, *more)
                    continue

                def last(at, here=here, more=more):
                    total = here[at].astype(F32)
                    for one in more:
                        total += one[at].astype(F32)
                    total = total.astype(BF16)
                    here[at] = total
                    square = total.astype(F32)
                    square = square * square
                    rows, columns = square.shape
                    acc[...] += sum(square[a : a + 8, b : b + 128] for a in range(0, rows, 8) for b in range(0, columns, 128))

                tiles(i, last)
            if q < side - 1:
                for c in COLOURS:
                    pl.semaphore_wait(cred2.at[c], 1)
                    copy(buf(0, c, q, i), buf(1, c, q, i), ss.at[1, c, q, i], rs.at[1, c, q, i], along_b(c, 1)).start()

    sq[me] = acc[...]

    def sq_copy(k):
        return copy(sq.at[me], sq.at[me], sq_ss.at[k], sq_rs.at[k], lax.rem(me + k, n))

    for k in range(1, n):
        sq_copy(k).start()
    for k in range(1, n):
        sq_copy(k).wait()
    total = sum(sq[k] for k in range(n))
    total = jnp.sum(total, axis=(0, 1), keepdims=True)
    factor = jnp.minimum(1.0, 0.5 * lax.rsqrt(total / count + 1e-30))
    factor_ref[...] = jnp.broadcast_to(factor, factor_ref.shape)

    last_own = (3 * side) % 2

    def out(c, j, rows):
        if rows:
            ref, layer = pick(4, c)
            return ref.at[layer, j]
        return o_down.at[:, j, :, cols(c)]

    for i in range(kinds):
        for c in COLOURS:
            rows = i < PIECES
            pltpu.make_async_copy(source(1, w_down, c, me, i), own(last_own, c, i), own_sem.at[last_own, c, i]).wait()
            for cp in mv_load(c, i):
                cp.wait()
            w_ref, g_ref = own(last_own, c, i), buf(0, c, side - 1, i)
            m_ref = mr.at[c, i % 2] if rows else mc.at[c, i - PIECES]
            v_ref = vr.at[c, i % 2] if rows else vc.at[c, i - PIECES]

            def body(at, w_ref=w_ref, g_ref=g_ref, m_ref=m_ref, v_ref=v_ref):
                g = g_ref[at].astype(F32) * factor
                m, v = moments(m_ref[at], v_ref[at], g)
                w_ref[at] = new_weight(w_ref[at].astype(F32), m, v)

            tiles(i, body)
            if i + 2 < PIECES:
                for cp in mv_load(c, i + 2):
                    cp.start()
            kind = 0 if rows else 1
            there = source(4, o_down, c, me, i)
            copy(w_ref, there, ags_own.at[0, c, i], agr_own.at[0, c, i], along_b(c, 1)).start()
            copy(w_ref, there, ags_own.at[1, c, i], agr_own.at[1, c, i], along_a(c, 1)).start()
            pltpu.make_async_copy(w_ref, there, loc_sem.at[0, c, i]).start()
            og = pick(5, c)[0].at[pick(5, c)[1], i] if rows else og_down.at[i - PIECES, :, cols(c)]
            pltpu.make_async_copy(g_ref, og, loc_sem.at[1, c, i]).start()

    for hop in range(1, side):
        for rows in (True, False):
            kind = 0 if rows else 1
            for c in COLOURS:
                here = out(c, block(c, 0, hop), rows)
                if hop == 1:
                    for i in range(kinds):
                        if (i < PIECES) == rows:
                            got(own(last_own, c, i), agr_own.at[0, c, i])
                else:
                    got(here, agr_a.at[hop, c, kind])
                if hop < side - 1:
                    copy(here, here, ags_a.at[hop + 1, c, kind], agr_a.at[hop + 1, c, kind], along_b(c, 1)).start()
                copy(here, here, ags_b.at[0, c, hop, kind], agr_b.at[0, c, hop, kind], along_a(c, 1)).start()
    for hop in range(1, side):
        for q in range(side):
            for rows in (True, False):
                kind = 0 if rows else 1
                for c in COLOURS:
                    here = out(c, block(c, hop, q), rows)
                    if hop == 1 and q == 0:
                        for i in range(kinds):
                            if (i < PIECES) == rows:
                                got(own(last_own, c, i), agr_own.at[1, c, i])
                    else:
                        got(here, agr_b.at[hop - 1, c, q, kind])
                    if hop < side - 1:
                        copy(here, here, ags_b.at[hop, c, q, kind], agr_b.at[hop, c, q, kind], along_a(c, 1)).start()

    for c in COLOURS:
        for i in range(kinds):
            for k in range(2):
                got(own(last_own, c, i), ags_own.at[k, c, i])
                got(own(last_own, c, i), loc_sem.at[k, c, i])
        for rows in (True, False):
            kind = 0 if rows else 1
            here = out(c, me, rows)
            for hop in range(2, side):
                got(here, ags_a.at[hop, c, kind])
            for hop in range(side - 1):
                for q in range(side):
                    if (hop, q) != (0, 0):
                        got(here, ags_b.at[hop, c, q, kind])


def solution(mesh):
    n = mesh.shape["dp"]
    side = math.isqrt(n)

    def step(*arrays):
        terms, weights, m, v = (arrays[i : i + 3] for i in (0, 3, 6, 9))
        layers, rows, wide = m[0].shape
        tall, narrow = m[2].shape[1:]
        assert side * side == n and layers * 2 == len(COLOURS), (n, layers)
        r, quarter = rows // PIECES, narrow // len(COLOURS)
        kinds = PIECES + layers

        def cut(whole):
            a, b, c = (w.reshape(layers, n, *shape) for w, shape in zip(whole, ((PIECES, r, wide),) * 2 + ((tall, narrow),), strict=True))
            return a, b, c

        def cut_own(blocks):
            return (*(one.reshape(layers, PIECES, r, wide) for one in blocks[:2]), blocks[2])

        args = (*cut([t[0] for t in terms]), *cut(weights), *cut_own(m), *cut_own(v))
        whole_shapes = [jax.ShapeDtypeStruct((layers, n, PIECES, r, wide), BF16)] * 2 + [jax.ShapeDtypeStruct((layers, n, tall, narrow), BF16)]
        own_shapes = [jax.ShapeDtypeStruct((layers, PIECES, r, wide), BF16)] * 2 + [jax.ShapeDtypeStruct((layers, tall, narrow), BF16)]
        count = float(n * sum(one.size for one in m))
        dma = pltpu.SemaphoreType.DMA
        anywhere = pl.BlockSpec(memory_space=pl.ANY)
        results = pl.pallas_call(
            functools.partial(kernel, n, side, count),
            name="sum_step_gather",
            out_shape=(*whole_shapes, *own_shapes, jax.ShapeDtypeStruct((8, 128), F32)),
            in_specs=[anywhere] * 12,
            out_specs=[anywhere] * 6 + [pl.BlockSpec(memory_space=pltpu.VMEM)],
            scratch_shapes=[
                pltpu.VMEM((2, 4, side, PIECES, r, wide), BF16),
                pltpu.VMEM((2, 4, side, layers, tall, quarter), BF16),
                pltpu.VMEM((2, 4, PIECES, r, wide), BF16),
                pltpu.VMEM((2, 4, layers, tall, quarter), BF16),
                pltpu.VMEM((4, 2, r, wide), F32),
                pltpu.VMEM((4, layers, tall, quarter), F32),
                pltpu.VMEM((4, 2, r, wide), F32),
                pltpu.VMEM((4, layers, tall, quarter), F32),
                pltpu.VMEM((8, 128), F32),
                pltpu.VMEM((n, 8, 128), F32),
                dma((2, 4, side, kinds)),
                dma((2, 4, side, kinds)),
                dma((2, 4, kinds)),
                dma((2, 4, kinds)),
                pltpu.SemaphoreType.REGULAR((4,)),
                pltpu.SemaphoreType.REGULAR((4,)),
                dma((n,)),
                dma((n,)),
                dma((2, 4, kinds)),
                dma((side, 4, 2)),
                dma((side, 4, 2)),
                dma((side, 4, side, 2)),
                dma((side, 4, side, 2)),
                dma((2, 4, kinds)),
                dma((2, 4, kinds)),
            ],
            compiler_params=pltpu.CompilerParams(collective_id=0, has_side_effects=True, vmem_limit_bytes=66_000_000),
        )(*args)
        new_w = [one.reshape(w.shape) for one, w in zip(results[:3], weights, strict=True)]
        g = [one.reshape(old.shape).astype(F32) * results[6][0, 0] for one, old in zip(results[3:6], m, strict=True)]
        new = [moments(*one) for one in zip(m, v, g, strict=True)]
        return (*new_w, *(one[0] for one in new), *(one[1] for one in new))

    all_of, part = P(None, None, None), P(None, "dp", None)
    return jax.shard_map(
        step,
        mesh=mesh,
        in_specs=(P(("rep", "dp"), None, None, None),) * 3 + (all_of,) * 3 + (part,) * 6,
        out_specs=(P("rep", None, None),) * 3 + (P("rep", "dp", None),) * 6,
        check_vma=False,
    )
```

time: 1200 us -> 883 us (0.74)
  waiting for transfers between devices: 1070 us -> 0 us
  Pallas kernels: 0 us -> 806 us
  blocking collectives: 31.7 us -> 0 us
  between operations: 17.5 us -> 0.78 us
    pallas_call x0 -> x1, Pallas kernels: none -> 806 us  [step(): pl.pallas_call(functools.partial(kernel, n, side, count), name='sum_step_...]
    all_gather x3 -> x0, waiting for transfers between devices: 454 us -> none  [step(): whole = [lax.all_gather(one[0], 'dp', axis=1, tiled=True) for one in new]]
    unnamed x7 -> x0, waiting for transfers between devices: 309 us -> none
    reduce_scatter x2 -> x0, waiting for transfers between devices: 304 us -> none  [step(): lax.psum_scatter(t[0], 'dp', scatter_dimension=1, tiled=True)]
    psum x1 -> x0, blocking collectives: 31.7 us -> none  [step(): squares = lax.psum(sum((jnp.sum(g * g) for g in gradients)), 'dp')]
    add x0 -> x3, other arithmetic: none -> 22 us  [moments(): v = 0.95 * v + 0.05 * g * g]
    convert_element_type x3 -> x0, other arithmetic: 18.2 us -> none  [adamw(): return ((w - 0.02 * step).astype(jnp.bfloat16), m, v)]
    unnamed x24 -> x33, local copies, waits for them, and re-layouts: 56.2 us -> 45.9 us
  transfers between devices with their start and end apart: 6 -> 0, of which waited for: 6 -> 0; matrix products, arithmetic and copies ran while one was open for 2% -> 0% of each run, Pallas kernels for 0% -> 0%
where the time goes in v1:
time: 883 us; the launch traced here: 882 us
  Pallas kernels  806 us (91%)
  local copies, waits for them, and re-layouts  47.1 us (5%)
  other arithmetic  27.2 us (3%)
    pallas_call x1, Pallas kernels, step(): pl.pallas_call(functools.partial(kernel, n, side, count), name='sum_step_...  806 us
    unnamed x33, local copies, waits for them, and re-layouts  45.9 us
    add x3, other arithmetic, moments(): v = 0.95 * v + 0.05 * g * g  22 us

profile of v1, /device:TPU:97, one launch (start us, length us, event | category | flops | bytes accessed | tf_op | source)
XLA Modules:
  0.0 881.6 jit_solution(12562751466296417122)
XLA Ops:
  0.6 806.5 %sum_step_gather.1 = (bf16[2,16,4,24,4224]{4,3,2,1,0:T(8,128)(2,1)}, bf16[2,16,4,24,4224]{4,3,2,1,0:T(8,128)(2,1)}, bf16[2,16,264,1536]{3,2,1,0:T(8,128)(2,1)}, ...) custom-call(bf16[2,16,4,24,4224]{4,3,2,1,0:T(8,128)(2,1)} %bitcast.2, ...), custom_call_target="tpu_custom_call" | custom-call | tf_op jit(solution)/shard_map/sum_step_gather/pallas_call | solution.py:346
  807.1 1.2 slice.2
  808.3 0.0 copy-start
  808.3 0.0 slice-start.7
  808.3 0.0 slice-start.8
  808.3 5.2 convert_multiply_fusion.1
  813.6 0.0 copy-done
  813.6 0.0 slice-start.9
  813.6 0.0 slice-start.10
  813.6 6.0 fusion
  819.6 0.0 slice-start.11
  819.6 0.0 slice-start.12
  819.6 7.6 fusion.1
  827.2 0.0 slice-start.13
  827.2 8.3 fusion.2
  835.5 0.0 slice-done.7
  835.5 0.0 slice-done.8
  835.5 0.0 slice-done.9
  835.6 0.0 slice-done.10
  835.6 0.0 slice-done.11
  835.6 0.0 slice-done.12
  835.6 0.0 slice-done.13
  835.6 0.0 slice-start
  835.6 0.0 slice-start.1
  835.6 0.0 slice-start.2
  835.6 0.0 slice-start.3
  835.6 13.1 %copy.24 = bf16[2,1536,4224]{2,1,0:T(8,128)(2,1)} copy(bf16[2,1536,4224]{2,1,0:T(8,128)(2,1)S(1)} %bitcast.36) | data formatting | bytes 51904512
  848.8 0.0 slice-start.4
  848.8 0.0 slice-start.5
  848.8 0.0 slice-start.6
  848.8 23.5 %copy.25 = bf16[2,1536,4224]{2,1,0:T(8,128)(2,1)} copy(bf16[2,1536,4224]{2,1,0:T(8,128)(2,1)} %bitcast.33) | data formatting | bytes 51904512
  872.3 0.0 slice-done
  872.3 0.0 slice-done.1
  872.3 0.0 slice-done.2
  872.3 0.0 slice-done.3
  872.3 0.0 slice-done.4
  872.3 0.0 slice-done.5
  872.4 0.0 slice-done.6
  872.4 9.2 %copy.26 = bf16[2,4224,1536]{2,1,0:T(8,128)(2,1)} copy(bf16[2,4224,1536]{2,1,0:T(8,128)(2,1)S(1)} %bitcast.32) | data formatting | bytes 51904512
  (2 shorter events, 0.0 us)
Async XLA Ops:
  808.3 5.2 copy-start
  808.3 27.2 %slice-start.7 = ((s8[25952256]{0:T(1024)(128)(4,1)}), s8[786432]{0:T(1024)(128)(4,1)S(1)}, s32[]{:S(2)}) async-start(s8[25952256]{0:T(1024)(128)(4,1)} %bitcast.34), calls=%async_computation.7 | async-start | bytes 1572864
  808.3 27.2 %slice-start.8 = ((s8[25952256]{0:T(1024)(128)(4,1)}), s8[4194304]{0:T(1024)(128)(4,1)S(1)}, s32[]{:S(2)}) async-start(s8[25952256]{0:T(1024)(128)(4,1)} %bitcast.34), calls=%async_computation.8 | async-start | bytes 8388608
  813.6 22.0 %slice-start.9 = ((s8[25952256]{0:T(1024)(128)(4,1)}), s8[4194304]{0:T(1024)(128)(4,1)S(1)}, s32[]{:S(2)}) async-start(s8[25952256]{0:T(1024)(128)(4,1)} %bitcast.34), calls=%async_computation.9 | async-start | bytes 8388608
  813.6 22.0 %slice-start.10 = ((s8[25952256]{0:T(1024)(128)(4,1)}), s8[4194304]{0:T(1024)(128)(4,1)S(1)}, s32[]{:S(2)}) async-start(s8[25952256]{0:T(1024)(128)(4,1)} %bitcast.34), calls=%async_computation.10 | async-start | bytes 8388608
  819.6 16.0 %slice-start.11 = ((s8[25952256]{0:T(1024)(128)(4,1)}), s8[4194304]{0:T(1024)(128)(4,1)S(1)}, s32[]{:S(2)}) async-start(s8[25952256]{0:T(1024)(128)(4,1)} %bitcast.34), calls=%async_computation.11 | async-start | bytes 8388608
  819.6 16.0 %slice-start.12 = ((s8[25952256]{0:T(1024)(128)(4,1)}), s8[4194304]{0:T(1024)(128)(4,1)S(1)}, s32[]{:S(2)}) async-start(s8[25952256]{0:T(1024)(128)(4,1)} %bitcast.34), calls=%async_computation.12 | async-start | bytes 8388608
  827.2 8.4 slice-start.13
  835.6 36.7 %slice-start = ((s8[25952256]{0:T(1024)(128)(4,1)}), s8[4194304]{0:T(1024)(128)(4,1)S(1)}, s32[]{:S(2)}) async-start(s8[25952256]{0:T(1024)(128)(4,1)} %bitcast.30), calls=%async_computation | async-start | bytes 8388608
  835.6 36.7 %slice-start.1 = ((s8[25952256]{0:T(1024)(128)(4,1)}), s8[4194304]{0:T(1024)(128)(4,1)S(1)}, s32[]{:S(2)}) async-start(s8[25952256]{0:T(1024)(128)(4,1)} %bitcast.30), calls=%async_computation.1 | async-start | bytes 8388608
  835.6 36.7 %slice-start.2 = ((s8[25952256]{0:T(1024)(128)(4,1)}), s8[4194304]{0:T(1024)(128)(4,1)S(1)}, s32[]{:S(2)}) async-start(s8[25952256]{0:T(1024)(128)(4,1)} %bitcast.30), calls=%async_computation.2 | async-start | bytes 8388608
  835.6 36.7 %slice-start.3 = ((s8[25952256]{0:T(1024)(128)(4,1)}), s8[4194304]{0:T(1024)(128)(4,1)S(1)}, s32[]{:S(2)}) async-start(s8[25952256]{0:T(1024)(128)(4,1)} %bitcast.30), calls=%async_computation.3 | async-start | bytes 8388608
  848.8 23.6 %slice-start.4 = ((s8[25952256]{0:T(1024)(128)(4,1)}), s8[4194304]{0:T(1024)(128)(4,1)S(1)}, s32[]{:S(2)}) async-start(s8[25952256]{0:T(1024)(128)(4,1)} %bitcast.30), calls=%async_computation.4 | async-start | bytes 8388608
  848.8 23.6 %slice-start.5 = ((s8[25952256]{0:T(1024)(128)(4,1)}), s8[4194304]{0:T(1024)(128)(4,1)S(1)}, s32[]{:S(2)}) async-start(s8[25952256]{0:T(1024)(128)(4,1)} %bitcast.30), calls=%async_computation.5 | async-start | bytes 8388608
  848.8 23.6 %slice-start.6 = ((s8[25952256]{0:T(1024)(128)(4,1)}), s8[786432]{0:T(1024)(128)(4,1)S(1)}, s32[]{:S(2)}) async-start(s8[25952256]{0:T(1024)(128)(4,1)} %bitcast.30), calls=%async_computation.6 | async-start | bytes 1572864
